TPU v7x, 256 devices: a whole 4x4x8 slice. The times are simulated.
256 devices in a mesh: gx: 8 (over y, core), gy: 8 (over x, z_hi), gz: 4 (over z_lo).
Axes of the slice: x: 4, y: 4, z: 8 (z_hi: 2, z_lo: 4; z = z_hi * 4 + z_lo), core: 2. Of those that a mesh axis runs over, the one named last changes fastest.
Arguments:
- rhs: float32 [3, 128, 256, 512], P(None, 'gx', 'gy', 'gz'), may hold values from -6 to 6
- viscous: float32 [8, 16, 32], P('gx', 'gy', 'gz'), may hold values from 0.3 to 3
- reaction: float32 [8, 16, 32], P('gx', 'gy', 'gz'), may hold values from 0.05 to 1
Outputs:
- correction: float32 [3, 128, 256, 512], P(None, 'gx', 'gy', 'gz')
All inputs are finite; a program needn't handle non-finite values.
Results may differ from a plain program's by a relative error of at most 0.00008.
Values sent between devices are 32-bit elements; how exact they have to be, the bound alone decides.
A program may use at most 64 MiB of HBM per device.

v0:
```python
import functools

import jax
import jax.numpy as jnp
import numpy as np
from jax import lax
from jax.experimental import pallas as pl
from jax.experimental.pallas import tpu as pltpu
from jax.sharding import PartitionSpec as P

EDGE = 16
SPAN = EDGE + 2
MODES = 384
ROWS = 160
MESH = pl.DeviceIdType.MESH
NT = (((1,), (1,)), ((), ()))
NN = (((1,), (0,)), ((), ()))
DIRS = [
    (dx, dy, dz)
    for dz in (0, -1, 1)
    for dy in (0, -1, 1)
    for dx in (0, -1, 1)
    if (dx, dy, dz) != (0, 0, 0)
]
Y_FIRST, Y_MID, Y_LAST, X_FIRST, X_LAST = 0, 16, 48, 64, 96


def tables():
    i = np.arange(SPAN)
    basis = np.sqrt(2.0 / (SPAN + 1)) * np.sin(np.pi * np.outer(i + 1, i + 1) / (SPAN + 1))
    lam = 2.0 - 2.0 * np.cos(np.pi * (i + 1) / (SPAN + 1))
    nz = 8
    z_fwd = np.zeros((ROWS, 128))
    z_back = np.zeros((nz * SPAN, 128))
    for h in range(nz):
        for z in range(128):
            w = z - EDGE * h + 1
            if 0 <= w < SPAN:
                z_fwd[h * SPAN : (h + 1) * SPAN, z] = basis[w]
            if 1 <= w <= EDGE:
                z_back[h * SPAN : (h + 1) * SPAN, z] = basis[w]
    z_fwd[nz * SPAN, 0] = 1.0
    z_fwd[nz * SPAN + 1, 127] = 1.0
    pair = np.zeros((SPAN, SPAN, MODES))
    for a in range(SPAN):
        for b in range(SPAN):
            pair[a, b, : SPAN * SPAN] = np.outer(basis[a], basis[b]).reshape(-1)
    main = pair[1:17, 1:17].reshape(256, MODES)
    shell = np.zeros((2, 128, MODES))
    for x in range(16):
        shell[0, Y_LAST + x] = pair[x + 1, 0]
        shell[0, 32 + x] = pair[x + 1, 17]
        shell[1, Y_FIRST + x] = pair[x + 1, 17]
        shell[1, Y_MID + x] = pair[x + 1, 0]
    for y in range(17):
        shell[0, X_FIRST + y] = pair[17, y + 1]
        shell[0, X_LAST + y] = pair[0, y + 1]
        shell[1, X_FIRST + 31 - y] = pair[17, 16 - y]
        shell[1, X_LAST + 31 - y] = pair[0, 16 - y]
    shell[0, X_FIRST + 31], shell[0, X_LAST + 31] = pair[17, 0], pair[0, 0]
    shell[1, X_FIRST], shell[1, X_LAST] = pair[17, 17], pair[0, 17]
    q = np.arange(nz * SPAN)
    first = np.where(q < SPAN, basis[0][q % SPAN], 0.0)
    last = np.where(q >= (nz - 1) * SPAN, basis[17][q % SPAN], 0.0)
    lam_z = lam[q % SPAN]
    columns = np.stack([np.repeat(v[:, None], 128, 1) for v in (first, last, lam_z)])
    lam_xy = np.zeros((8, MODES))
    lam_xy[:, : SPAN * SPAN] = (lam[:, None] + lam[None, :]).reshape(-1)
    f32 = functools.partial(np.asarray, dtype=np.float32)
    return f32(z_fwd), f32(z_back), f32(main), f32(shell), f32(columns), f32(lam_xy)


def halves(x):
    hi = x.astype(jnp.bfloat16)
    return hi, (x - hi.astype(jnp.float32)).astype(jnp.bfloat16)


def table_halves(x):
    hi = x.astype(jnp.bfloat16)
    return hi, (x - hi.astype(np.float32)).astype(jnp.bfloat16)


def constants():
    z_fwd, z_back, main, shell, columns, lam_xy = tables()
    zh, zl = table_halves(z_fwd)
    bh, bl = table_halves(z_back)
    mh, ml = table_halves(main)
    sh, sl = table_halves(shell)
    return (
        np.concatenate([zh, zh, zl], axis=1),
        np.stack([bh, bl]),
        np.concatenate([mh, mh, ml], axis=0),
        np.concatenate([sh, sh, sl], axis=1),
        np.concatenate([mh, mh, ml], axis=1),
        columns,
        lam_xy,
    )


def dot(a, b, dims):
    return lax.dot_general(a, b, dims, preferred_element_type=jnp.float32)


def kernel(
    sizes, rhs_hbm, visc_ref, reac_ref, zf_hbm, zb_hbm, km_hbm, ks_hbm, kb_hbm, col_hbm, lam_hbm,
    out_ref,
    rhs, first, resid, face, face_f, corner, zface, zedge,
    rx, ry, rc, rz, re, shell, z1h, z1l, inv,
    zf, zb, km, ks, kb, col, lam, load_sem, send_sem, recv_sem,
):
    axes = ("gx", "gy", "gz")
    me = tuple(lax.axis_index(a) for a in axes)

    def exists(d):
        ok = None
        for p, n, s in zip(me, sizes, d):
            if s:
                c = (p + s >= 0) & (p + s < n)
                ok = c if ok is None else ok & c
        return ok

    def peer(d):
        return tuple(p + s for p, s in zip(me, d))

    def minus(d):
        return tuple(-s for s in d)

    barrier = pltpu.get_barrier_semaphore()
    count = jnp.int32(0)
    for d in DIRS:
        ok = exists(d)
        count = count + ok.astype(jnp.int32)

        @pl.when(ok)
        def _(d=d):
            pl.semaphore_signal(barrier, inc=1, device_id=peer(d), device_id_type=MESH)

    loads = []
    for k, (src, dst) in enumerate(
        [(rhs_hbm, rhs), (zf_hbm, zf), (km_hbm, km), (ks_hbm, ks), (col_hbm, col), (lam_hbm, lam),
         (kb_hbm, kb), (zb_hbm, zb)]
    ):
        loads.append(pltpu.make_async_copy(src, dst, load_sem.at[k]))
        loads[-1].start()

    def pieces(rnd, d, face_ref):
        dx, dy, dz = d
        full = 0 if rnd == 0 else 1
        out = []
        if dz == 0 and dy == 0:
            lo = X_LAST if dx > 0 else X_FIRST
            out.append((face_ref.at[:, pl.ds(lo, 32), :], rx.at[rnd, int(dx > 0)]))
        elif dz == 0 and dx == 0:
            lo = Y_LAST if dy > 0 else Y_FIRST
            out.append((face_ref.at[:, pl.ds(lo, 16), :], ry.at[rnd, int(dy > 0)]))
        elif dz == 0:
            k = 2 * int(dx > 0) + int(dy > 0)
            out.append((corner.at[full, k], rc.at[full, k]))
        else:
            s = int(dz > 0)
            if dx == 0 and dy == 0:
                out.append((zface.at[rnd, s], rz.at[rnd, s]))
            if rnd != 1:
                out.append((zedge.at[full, s], re.at[full, s, 3 * (dx + 1) + dy + 1]))
        return out

    zface[...] = jnp.zeros(zface.shape, jnp.float32)
    started = {0: [], 1: [], 2: []}
    counter = [0]

    def send(rnd, dirs, face_ref):
        for d in dirs:
            copies = []
            for src, dst in pieces(rnd, d, face_ref):
                k = counter[0]
                counter[0] += 1
                copies.append(
                    pltpu.make_async_remote_copy(
                        src_ref=src, dst_ref=dst, send_sem=send_sem.at[k], recv_sem=recv_sem.at[k],
                        device_id=peer(d), device_id_type=MESH,
                    )
                )
                @pl.when(jnp.logical_not(exists(minus(d))))
                def _(dst=dst):
                    dst[...] = jnp.zeros(dst.shape, jnp.float32)

            @pl.when(exists(d))
            def _(copies=copies):
                for c in copies:
                    c.start()

            started[rnd].append((d, copies))

    def arrive(rnd):
        for d, copies in started[rnd]:
            @pl.when(exists(minus(d)))
            def _(copies=copies):
                for c in copies:
                    c.wait_recv()

    def drain(rnd):
        for d, copies in started[rnd]:
            @pl.when(exists(d))
            def _(copies=copies):
                for c in copies:
                    c.wait_send()

    def fill_face(src, dst):
        for c in range(3):
            for k, y in enumerate((0, 15, 16, 31)):
                dst[c, 16 * k : 16 * k + 16, :] = src[c, pl.ds(y, 16, stride=32), :]
            dst[c, X_FIRST : X_FIRST + 32, :] = src[c, 0:32]
            dst[c, X_LAST : X_LAST + 32, :] = src[c, 480:512]

    def fill_corner(full, face_ref):
        for k, row in enumerate((X_FIRST, X_FIRST + 31, X_LAST, X_LAST + 31)):
            for c in range(3):
                corner[full, k, c] = face_ref[c, row : row + 1, :]

    def z_forward(x):
        hi, lo = halves(x)
        two = jnp.concatenate([hi, lo], axis=1)
        return dot(zf[:, :256], two, NT) + dot(zf[:, 256:], hi, NT)

    def z_ends(x):
        hi, lo = halves(x)
        two = jnp.concatenate([hi, lo], axis=1)
        return dot(zf[144:, :256], two, NT)

    def store_halves(c, f, rows, lanes, x):
        hi, lo = halves(x)
        z1h[2 * c + f, rows, lanes] = hi
        z1l[2 * c + f, rows, lanes] = lo

    def main_part(src, rnd):
        def step(c, _):
            block = src[c].reshape(16, 32, 128)
            for f in range(2):
                m = z_forward(block[:, 16 * f : 16 * f + 16].reshape(256, 128))
                store_halves(c, f, slice(0, 144), slice(0, 256), m[:144])
                for s in range(2):
                    zface[rnd, s, pl.ds(2 * c + f, 1), :] = m[144 + s : 145 + s]
            return 0

        lax.fori_loop(0, 3, step, 0)

    def edges(full, face_ref):
        e = z_ends(face_ref[...].reshape(384, 128))
        for s in range(2):
            for c in range(3):
                zedge[full, s, c] = e[s : s + 1, 128 * c : 128 * c + 128]

    lane = lax.broadcasted_iota(jnp.int32, (1, 128), 1)

    def shells(full, rnd, face_ref):
        for c in range(3):
            for f in range(2):
                s = shell.at[c, f]
                s[0:16] = ry[rnd, 0, c]
                s[16:48] = face_ref[c, 16:48]
                s[48:64] = ry[rnd, 1, c]
                s[64:96] = rx[rnd, 0, c]
                s[96:128] = rx[rnd, 1, c]
                if f == 0:
                    s[95:96] = rc[full, 1, c]
                    s[127:128] = rc[full, 3, c]
                else:
                    s[64:65] = rc[full, 0, c]
                    s[96:97] = rc[full, 2, c]

    def slot(d):
        return 3 * (d[0] + 1) + d[1] + 1

    def shell_part(full, rnd):
        def step(c, _):
            m = z_forward(shell[c].reshape(256, 128))
            for f in range(2):
                store_halves(c, f, slice(0, 144), slice(256, 384), m[:144, 128 * f : 128 * f + 128])
            for f in range(2):
                main, ring = [], []
                for s in (1, 0):
                    main.append(rz[rnd, s, pl.ds(2 * c + f, 1), :])
                    got = lambda dx, dy: re[full, s, slot((dx, dy)), c]
                    t = got(0, 0)
                    if f == 0:
                        t = jnp.where((lane >= 48) & (lane < 64), got(0, 1), t)
                        t = jnp.where((lane >= 64) & (lane < 95), got(-1, 0), t)
                        t = jnp.where(lane == 95, got(-1, 1), t)
                        t = jnp.where((lane >= 96) & (lane < 127), got(1, 0), t)
                        t = jnp.where(lane == 127, got(1, 1), t)
                    else:
                        t = jnp.where(lane < 16, got(0, -1), t)
                        t = jnp.where(lane == 64, got(-1, -1), t)
                        t = jnp.where((lane > 64) & (lane < 96), got(-1, 0), t)
                        t = jnp.where(lane == 96, got(1, -1), t)
                        t = jnp.where(lane > 96, got(1, 0), t)
                    ring.append(t)
                pad = jnp.zeros((14, 384), jnp.float32)
                planes = jnp.concatenate(
                    [jnp.concatenate(main, axis=0), jnp.concatenate(ring, axis=0)], axis=1
                )
                planes = jnp.concatenate([planes, pad], axis=0)
                store_halves(c, f, slice(144, 160), slice(0, 384), planes)
            return 0

        lax.fori_loop(0, 3, step, 0)

    def joined(parts):
        return jnp.concatenate([p.reshape(16, 16, 128) for p in parts], axis=1).reshape(512, 128)

    def solve(put):
        def step(c, _):
            parts = []
            for f in range(2):
                k = 2 * c + f
                hi, lo = z1h[k], z1l[k]
                lhs = jnp.concatenate([hi[:, :256], lo[:, :256], hi[:, :256]], axis=1)
                ring = jnp.concatenate([hi[:, 256:], lo[:, 256:], hi[:, 256:]], axis=1)
                m = dot(lhs, km[...], NN) + dot(ring, ks[f], NN)
                wide = lambda v: jnp.concatenate([v] * 3, axis=1)
                t = m[:144] + wide(col[0]) * m[144:145] + wide(col[1]) * m[145:146]
                t = t * inv[f]
                hi, lo = halves(t)
                data = jnp.concatenate([hi, lo, hi], axis=1)
                u = dot(kb3(), data, NT)
                hi, lo = halves(u)
                parts.append(dot(hi, zb[0], NN) + dot(lo, zb[0], NN) + dot(hi, zb[1], NN))
            put(c, parts)
            return 0

        lax.fori_loop(0, 3, step, 0)

    def kb3():
        return kb[...]

    faces = [d for d in DIRS if sum(map(abs, d)) == 1]
    flat_dirs = [d for d in DIRS if d[2] == 0]
    z_dirs = [d for d in DIRS if d[2] != 0]

    loads[0].wait()
    fill_face(rhs, face.at[0])
    fill_corner(0, face.at[0])
    pl.semaphore_wait(barrier, count)
    send(0, flat_dirs, face.at[0])
    loads[1].wait()
    main_part(rhs, 0)
    edges(0, face.at[0])
    send(0, z_dirs, face.at[0])
    for k in range(2, 8):
        loads[k].wait()

    rows = lax.broadcasted_iota(jnp.int32, (144, 128), 0)
    for f in range(2):
        v = jnp.zeros((144, 128), jnp.float32)
        r = jnp.zeros((144, 128), jnp.float32)
        for h in range(8):
            at = (rows >= SPAN * h) & (rows < SPAN * h + SPAN)
            v = jnp.where(at, visc_ref[f, h], v)
            r = jnp.where(at, reac_ref[f, h], r)
        for t in range(3):
            part = slice(128 * t, 128 * t + 128)
            inv[f, :, part] = 1.0 / (v * (col[2] + lam[0:1, part]) + r)

    arrive(0)
    shells(0, 0, face.at[0])
    shell_part(0, 0)

    def put_first(c, parts):
        first[c] = joined(parts)

    solve(put_first)

    fill_face(first, face_f)
    flat_faces = [d for d in faces if d[2] == 0]
    send(1, flat_faces, face_f)

    def first_ends(c, _):
        block = first[c].reshape(16, 32, 128)
        for f in range(2):
            e = z_ends(block[:, 16 * f : 16 * f + 16].reshape(256, 128))
            for s in range(2):
                zface[1, s, pl.ds(2 * c + f, 1), :] = e[s : s + 1]
        return 0

    lax.fori_loop(0, 3, first_ends, 0)
    send(1, [d for d in faces if d[2] != 0], face_f)

    visc_z, reac_z = [], []
    for f in range(2):
        v = jnp.zeros((1, 128), jnp.float32)
        r = jnp.zeros((1, 128), jnp.float32)
        for h in range(8):
            at = (lane >= EDGE * h) & (lane < EDGE * h + EDGE)
            v = jnp.where(at, visc_ref[f, h], v)
            r = jnp.where(at, reac_ref[f, h], r)
        visc_z.append(v)
        reac_z.append(r)

    arrive(1)
    drain(0)

    y_index = lax.broadcasted_iota(jnp.int32, (16, 32, 128), 1)
    z_index = lax.broadcasted_iota(jnp.int32, (16, 32, 128), 2)
    visc_b = jnp.where(y_index < 16, visc_z[0].reshape(1, 1, 128), visc_z[1].reshape(1, 1, 128))
    reac_b = jnp.where(y_index < 16, reac_z[0].reshape(1, 1, 128), reac_z[1].reshape(1, 1, 128))
    below = jnp.transpose(jnp.concatenate([rz[1, 1], rz[1, 0]], axis=0))
    for c in range(3):
        x = first[c].reshape(16, 32, 128)
        beside = jnp.concatenate([rx[1, 1, c][None], x[:15]], axis=0)
        beside = beside + jnp.concatenate([x[1:], rx[1, 0, c][None]], axis=0)
        ylo, yhi = (jnp.broadcast_to(ry[1, s, c][:, None, :], (16, 32, 128)) for s in (1, 0))
        beside = beside + jnp.where(y_index == 0, ylo, pltpu.roll(x, 1, 1))
        beside = beside + jnp.where(y_index == 31, yhi, pltpu.roll(x, 31, 1))
        zlo, zhi = (
            jnp.concatenate(
                [
                    jnp.broadcast_to(below[:, k : k + 1], (256, 128)).reshape(16, 16, 128)
                    for k in (8 * s + 2 * c, 8 * s + 2 * c + 1)
                ],
                axis=1,
            )
            for s in (0, 1)
        )
        beside = beside + jnp.where(z_index == 0, zlo, pltpu.roll(x, 1, 2))
        beside = beside + jnp.where(z_index == 127, zhi, pltpu.roll(x, 127, 2))
        applied = reac_b * x + visc_b * (6.0 * x - beside)
        resid[c] = rhs[c] - applied.reshape(512, 128)

    fill_face(resid, face.at[1])
    fill_corner(1, face.at[1])
    send(2, flat_dirs, face.at[1])
    main_part(resid, 2)
    edges(1, face.at[1])
    send(2, z_dirs, face.at[1])
    drain(1)
    arrive(2)
    shells(1, 2, face.at[1])
    shell_part(1, 2)

    def put_last(c, parts):
        out_ref[c] = first[c] + joined(parts)

    solve(put_last)
    drain(2)


def shards(sizes, rhs, viscous, reaction):
    f32, bf16 = jnp.float32, jnp.bfloat16
    consts = constants()
    any_space = pl.BlockSpec(memory_space=pl.ANY)
    smem = pl.BlockSpec(memory_space=pltpu.SMEM)
    vmem = pl.BlockSpec(memory_space=pltpu.VMEM)
    copies = 28 * 2 + 6
    scratch = [
        pltpu.VMEM((3, 512, 128), f32),
        pltpu.VMEM((3, 512, 128), f32),
        pltpu.VMEM((3, 512, 128), f32),
        pltpu.VMEM((2, 3, 128, 128), f32),
        pltpu.VMEM((3, 128, 128), f32),
        pltpu.VMEM((2, 4, 3, 1, 128), f32),
        pltpu.VMEM((3, 2, 8, 256), f32),
        pltpu.VMEM((2, 2, 3, 1, 128), f32),
        pltpu.VMEM((3, 2, 3, 32, 128), f32),
        pltpu.VMEM((3, 2, 3, 16, 128), f32),
        pltpu.VMEM((2, 4, 3, 1, 128), f32),
        pltpu.VMEM((3, 2, 8, 256), f32),
        pltpu.VMEM((2, 2, 9, 3, 1, 128), f32),
        pltpu.VMEM((3, 2, 128, 128), f32),
        pltpu.VMEM((6, ROWS, MODES), bf16),
        pltpu.VMEM((6, ROWS, MODES), bf16),
        pltpu.VMEM((2, 144, MODES), f32),
    ]
    scratch += [pltpu.VMEM(t.shape, t.dtype) for t in consts]
    scratch += [
        pltpu.SemaphoreType.DMA((8,)),
        pltpu.SemaphoreType.DMA((copies,)),
        pltpu.SemaphoreType.DMA((copies,)),
    ]
    out = pl.pallas_call(
        functools.partial(kernel, sizes),
        out_shape=jax.ShapeDtypeStruct((3, 512, 128), f32),
        in_specs=[any_space, smem, smem] + [any_space] * len(consts),
        out_specs=vmem,
        scratch_shapes=scratch,
        compiler_params=pltpu.CompilerParams(
            collective_id=0, has_side_effects=True, vmem_limit_bytes=48 * 2**20
        ),
    )(rhs.reshape(3, 512, 128), viscous.reshape(2, 8), reaction.reshape(2, 8), *consts)
    return out.reshape(rhs.shape)


def solution(mesh):
    sizes = tuple(mesh.shape[a] for a in ("gx", "gy", "gz"))
    placed = (P(None, "gx", "gy", "gz"), P("gx", "gy", "gz"), P("gx", "gy", "gz"))
    return jax.shard_map(
        functools.partial(shards, sizes),
        mesh=mesh,
        in_specs=placed,
        out_specs=P(None, "gx", "gy", "gz"),
        check_vma=False,
    )
```

profile of v0, /device:TPU:1, one launch (start us, length us, event | category | flops | bytes accessed | tf_op | source)
XLA Modules:
  0.0 52.4 jit_solution(10746480834285772981)
XLA Ops:
  0.0 0.0 copy-start.7
  0.0 0.0 copy-start.9
  0.0 0.0 copy-start.8
  0.0 0.7 %copy-done.7 = f32[8,384]{1,0:T(8,128)S(1)} copy-done((f32[8,384]{1,0:T(8,128)S(1)}, f32[8,384]{1,0:T(8,128)}, u32[]{:S(2)}) %copy-start.7) | copy-done | bytes 12312
  0.7 0.0 copy-done.9
  0.7 0.0 copy-done.8
  0.7 0.0 copy-start
  0.7 1.1 %copy-done = f32[3,16,32,128]{3,2,1,0:T(8,128)S(1)} copy-done((f32[3,16,32,128]{3,2,1,0:T(8,128)S(1)}, f32[3,16,32,128]{3,2,1,0:T(8,128)}, u32[]{:S(2)}) %copy-start) | copy-done | bytes 786456
  1.8 0.0 copy-start.1
  1.9 1.1 %copy-done.1 = bf16[256,1152]{1,0:T(8,128)(2,1)S(1)} copy-done((bf16[256,1152]{1,0:T(8,128)(2,1)S(1)}, bf16[256,1152]{1,0:T(8,128)(2,1)}, u32[]{:S(2)}) %copy-start.1) | copy-done | bytes 589848
  2.9 0.0 copy-start.2
  2.9 1.1 %copy-done.2 = bf16[2,384,384]{2,1,0:T(8,128)(2,1)S(1)} copy-done((bf16[2,384,384]{2,1,0:T(8,128)(2,1)S(1)}, bf16[2,384,384]{2,1,0:T(8,128)(2,1)}, u32[]{:S(2)}) %copy-start.2) | copy-done | bytes 589848
  4.0 0.0 copy-start.3
  4.0 1.1 %copy-done.3 = bf16[768,384]{1,0:T(8,128)(2,1)S(1)} copy-done((bf16[768,384]{1,0:T(8,128)(2,1)S(1)}, bf16[768,384]{1,0:T(8,128)(2,1)}, u32[]{:S(2)}) %copy-start.3) | copy-done | bytes 589848
  5.0 0.0 copy-start.4
  5.0 0.9 %copy-done.4 = f32[3,144,128]{2,1,0:T(8,128)S(1)} copy-done((f32[3,144,128]{2,1,0:T(8,128)S(1)}, f32[3,144,128]{2,1,0:T(8,128)}, u32[]{:S(2)}) %copy-start.4) | copy-done | bytes 221208
  6.0 0.0 copy-start.5
  6.0 0.9 %copy-done.5 = bf16[160,384]{1,0:T(8,128)(2,1)S(1)} copy-done((bf16[160,384]{1,0:T(8,128)(2,1)S(1)}, bf16[160,384]{1,0:T(8,128)(2,1)}, u32[]{:S(2)}) %copy-start.5) | copy-done | bytes 122904
  6.9 0.0 copy-start.6
  6.9 0.9 %copy-done.6 = bf16[2,144,128]{2,1,0:T(8,128)(2,1)S(1)} copy-done((bf16[2,144,128]{2,1,0:T(8,128)(2,1)S(1)}, bf16[2,144,128]{2,1,0:T(8,128)(2,1)}, u32[]{:S(2)}) %copy-start.6) | copy-done | bytes 73752
  7.8 43.7 %shard_map.100 = f32[3,512,128]{2,1,0:T(8,128)S(1)} custom-call(f32[3,512,128]{2,1,0:T(8,128)S(1)} %bitcast.5, f32[2,8]{1,0:T(2,128)S(1)} %bitcast.6, f32[2,8]{1,0:T(2,128)S(1)} %bitcast.7, bf16[160,384]{1,0:T(8,128)(2,1)S(1)} %copy-done.5, bf16[2,144,128]{2,1,0:T(8,128)(2,1)S(1)} %copy-done.6, bf16[768,384]{1,0:T(8,128)(2,1)S(1)} %copy-done.3, ...), custom_call_target="tpu_custom_call" | custom-call | tf_op jit(solution)/shard_map/pallas_call | solution.py:479
  51.5 0.9 %copy.12 = f32[3,16,32,128]{3,2,1,0:T(8,128)} copy(f32[3,16,32,128]{3,2,1,0:T(8,128)S(1)} %bitcast.4) | data formatting | bytes 1572864
Async XLA Ops:
  0.0 0.7 %copy-start.7 = (f32[8,384]{1,0:T(8,128)S(1)}, f32[8,384]{1,0:T(8,128)}, u32[]{:S(2)}) copy-start(f32[8,384]{1,0:T(8,128)} %constant.20.clone.lam_hbm) | copy-start | bytes 36868
  0.0 0.7 %copy-start.9 = (f32[1,2,8]{2,1,0:T(2,128)S(1)}, f32[1,2,8]{2,1,0:T(2,128)}, u32[]{:S(2)}) copy-start(f32[1,2,8]{2,1,0:T(2,128)} %param.12) | copy-start | bytes 196
  0.0 0.7 %copy-start.8 = (f32[1,2,8]{2,1,0:T(2,128)S(1)}, f32[1,2,8]{2,1,0:T(2,128)}, u32[]{:S(2)}) copy-start(f32[1,2,8]{2,1,0:T(2,128)} %param.11) | copy-start | bytes 196
  0.7 1.1 %copy-start = (f32[3,16,32,128]{3,2,1,0:T(8,128)S(1)}, f32[3,16,32,128]{3,2,1,0:T(8,128)}, u32[]{:S(2)}) copy-start(f32[3,16,32,128]{3,2,1,0:T(8,128)} %param.10) | copy-start | bytes 2359300
  1.8 1.1 %copy-start.1 = (bf16[256,1152]{1,0:T(8,128)(2,1)S(1)}, bf16[256,1152]{1,0:T(8,128)(2,1)}, u32[]{:S(2)}) copy-start(bf16[256,1152]{1,0:T(8,128)(2,1)} %constant.18.clone.kb_hbm) | copy-start | bytes 1769476
  2.9 1.1 %copy-start.2 = (bf16[2,384,384]{2,1,0:T(8,128)(2,1)S(1)}, bf16[2,384,384]{2,1,0:T(8,128)(2,1)}, u32[]{:S(2)}) copy-start(bf16[2,384,384]{2,1,0:T(8,128)(2,1)} %constant.17.clone.ks_hbm) | copy-start | bytes 1769476
  4.0 1.1 %copy-start.3 = (bf16[768,384]{1,0:T(8,128)(2,1)S(1)}, bf16[768,384]{1,0:T(8,128)(2,1)}, u32[]{:S(2)}) copy-start(bf16[768,384]{1,0:T(8,128)(2,1)} %constant.16.clone.km_hbm) | copy-start | bytes 1769476
  5.0 0.9 %copy-start.4 = (f32[3,144,128]{2,1,0:T(8,128)S(1)}, f32[3,144,128]{2,1,0:T(8,128)}, u32[]{:S(2)}) copy-start(f32[3,144,128]{2,1,0:T(8,128)} %constant.19.clone.col_hbm) | copy-start | bytes 663556
  6.0 0.9 %copy-start.5 = (bf16[160,384]{1,0:T(8,128)(2,1)S(1)}, bf16[160,384]{1,0:T(8,128)(2,1)}, u32[]{:S(2)}) copy-start(bf16[160,384]{1,0:T(8,128)(2,1)} %constant.14.clone.zf_hbm) | copy-start | bytes 368644
  6.9 0.9 %copy-start.6 = (bf16[2,144,128]{2,1,0:T(8,128)(2,1)S(1)}, bf16[2,144,128]{2,1,0:T(8,128)(2,1)}, u32[]{:S(2)}) copy-start(bf16[2,144,128]{2,1,0:T(8,128)(2,1)} %constant.15.clone.zb_hbm) | copy-start | bytes 221188
where the time goes:
time: 53.1 us; the launch traced here: 52.4 us
  Pallas kernels  43.7 us (82%)
  local copies, waits for them, and re-layouts  8.63 us (16%)
    pallas_call x1, Pallas kernels, shards(): pl.pallas_call(functools.partial(kernel, sizes), out_shape=jax.ShapeDtype...  43.7 us
    unnamed x21, local copies, waits for them, and re-layouts  8.63 us

commit v1 on v0

--- a/solution.py
+++ b/solution.py
@@ -447,7 +447,7 @@
 def shards(sizes, rhs, viscous, reaction):
     f32, bf16 = jnp.float32, jnp.bfloat16
     consts = constants()
-    any_space = pl.BlockSpec(memory_space=pl.ANY)
+    any_space = pl.BlockSpec(memory_space=pltpu.HBM)
     smem = pl.BlockSpec(memory_space=pltpu.SMEM)
     vmem = pl.BlockSpec(memory_space=pltpu.VMEM)
     copies = 28 * 2 + 6
@@ -483,7 +483,7 @@
         out_specs=vmem,
         scratch_shapes=scratch,
         compiler_params=pltpu.CompilerParams(
-            collective_id=0, has_side_effects=True, vmem_limit_bytes=48 * 2**20
+            collective_id=0, has_side_effects=True, vmem_limit_bytes=67043328
         ),
     )(rhs.reshape(3, 512, 128), viscous.reshape(2, 8), reaction.reshape(2, 8), *consts)
     return out.reshape(rhs.shape)

time: 53.1 us -> 47.3 us (0.89)
  local copies, waits for them, and re-layouts: 8.63 us -> 2.06 us
  Pallas kernels: 43.7 us -> 44.8 us
    unnamed x21 -> x1, local copies, waits for them, and re-layouts: 8.63 us -> 2.06 us
    pallas_call x1, Pallas kernels: 43.7 us -> 44.8 us  [shards(): pl.pallas_call(functools.partial(kernel, sizes), out_shape=jax.ShapeDtype...]
where the time goes in v1:
time: 47.3 us; the launch traced here: 46.8 us
  Pallas kernels  44.8 us (95%)
  local copies, waits for them, and re-layouts  2.06 us (4%)
    pallas_call x1, Pallas kernels, shards(): pl.pallas_call(functools.partial(kernel, sizes), out_shape=jax.ShapeDtype...  44.8 us
    unnamed x1, local copies, waits for them, and re-layouts  2.06 us

profile of v1, /device:TPU:1, one launch (start us, length us, event | category | flops | bytes accessed | tf_op | source)
XLA Modules:
  0.0 46.8 jit_solution(1894815439358903883)
XLA Ops:
  0.0 44.8 %shard_map.100 = f32[3,512,128]{2,1,0:T(8,128)} custom-call(f32[3,512,128]{2,1,0:T(8,128)} %bitcast.5, f32[2,8]{1,0:T(2,128)} %bitcast.6, f32[2,8]{1,0:T(2,128)} %bitcast.7, bf16[160,384]{1,0:T(8,128)(2,1)} %constant.14.clone.zf_hbm, bf16[2,144,128]{2,1,0:T(8,128)(2,1)} %constant.15.clone.zb_hbm, bf16[768,384]{1,0:T(8,128)(2,1)} %constant.16.clone.km_hbm, ...), custom_call_target="tpu_custom_call" | custom-call | tf_op jit(solution)/shard_map/pallas_call | solution.py:479
  44.8 2.1 %copy.12 = f32[3,16,32,128]{3,2,1,0:T(8,128)} copy(f32[3,16,32,128]{3,2,1,0:T(8,128)} %bitcast.4) | data formatting | bytes 1572864
